TPU v7x, 32 devices: a whole 2x2x4 slice. The times are simulated.
32 devices in a mesh: wide: 8 (over y, x, core), narrow: 4 (over z).
Axes of the slice: x: 2, y: 2, z: 4, core: 2. Of those that a mesh axis runs over, the one named last changes fastest.
Arguments:
- tokens: bfloat16 [8192, 2048], P(('wide', 'narrow')), may hold values from -6 to 6
- out_grad: bfloat16 [8192, 2048], P(('wide', 'narrow')), may hold values from -6 to 6
- captions: bfloat16 [4096, 4096], P(('wide', 'narrow')), may hold values from -6 to 6
- image_blocks: int32 [32, 256], P('wide'), may hold values from 0 to 3, never falling along the last dimension, each value on 1 to 128 neighbouring positions
- caption_owner: int32 [8, 512], P('wide'), may hold values from 0 to 3, never falling along the last dimension, each value on 1 to 256 neighbouring positions
- norm_gains: float32 [3, 2048], replicated, may hold values from 0.25 to 1.75
- norm_shifts: float32 [3, 2048], replicated, may hold values from -3 to 3
- w_query: float32 [2048, 2048], P('wide', 'narrow'), may hold values from -0.125 to 0.125
- w_key: float32 [2048, 2048], P('wide', 'narrow'), may hold values from -0.125 to 0.125
- w_value: float32 [2048, 2048], P('wide', 'narrow'), may hold values from -0.125 to 0.125
- w_out: float32 [2048, 2048], P('narrow', 'wide'), may hold values from -0.375 to 0.375
- w_cross_query: float32 [2048, 2048], P('wide', 'narrow'), may hold values from -0.125 to 0.125
- w_cross_key: float32 [4096, 2048], P('wide', 'narrow'), may hold values from -0.09375 to 0.09375
- w_cross_value: float32 [4096, 2048], P('wide', 'narrow'), may hold values from -0.09375 to 0.09375
- w_cross_out: float32 [2048, 2048], P('narrow', 'wide'), may hold values from -0.375 to 0.375
- w_up: float32 [2048, 8192], P('wide', 'narrow'), may hold values from -0.125 to 0.125
- w_down: float32 [8192, 2048], P('narrow', 'wide'), may hold values from -0.0625 to 0.0625
Outputs:
- block_out: bfloat16 [8192, 2048], P(('wide', 'narrow'))
- grad_tokens: bfloat16 [8192, 2048], P(('wide', 'narrow'))
- grad_captions: bfloat16 [4096, 4096], P(('wide', 'narrow'))
- grad_norm_gains: float32 [3, 2048], replicated
- grad_norm_shifts: float32 [3, 2048], replicated
- grad_w_query: float32 [2048, 2048], P('wide', 'narrow')
- grad_w_key: float32 [2048, 2048], P('wide', 'narrow')
- grad_w_value: float32 [2048, 2048], P('wide', 'narrow')
- grad_w_out: float32 [2048, 2048], P('narrow', 'wide')
- grad_w_cross_query: float32 [2048, 2048], P('wide', 'narrow')
- grad_w_cross_key: float32 [4096, 2048], P('wide', 'narrow')
- grad_w_cross_value: float32 [4096, 2048], P('wide', 'narrow')
- grad_w_cross_out: float32 [2048, 2048], P('narrow', 'wide')
- grad_w_up: float32 [2048, 8192], P('wide', 'narrow')
- grad_w_down: float32 [8192, 2048], P('narrow', 'wide')
Inputs may be any that keep to these rules, and one draw needn't show every extreme that they name: `image_blocks`: within an image the block numbers never fall; each of the 4 blocks has 1 to 128 tokens, and one block of every image has exactly that many. `caption_owner`: within a group the owners never fall; every image of the group has 1 to 256 caption tokens, and one image of every group has exactly 256.
All inputs are finite; a program needn't handle non-finite values.
Results may differ from a plain program's by a relative error of at most 0.024.
Values may be sent and summed in bfloat16 or wider, within the bound.
A program may use at most 320 MiB of HBM per device.

v0:
```python
import jax
import jax.numpy as jnp
from jax import lax
from jax.sharding import PartitionSpec as P

HEAD_DIM = 128
PIX = 256
CHUNKS = 2
EPSILON = 1e-06
MASKED = -1000000000.0
BF = jnp.bfloat16
F32 = jnp.float32


def product(left_side, right_side):
    return lax.dot_general(
        left_side, right_side, (((left_side.ndim - 1,), (0,)), ((), ())), preferred_element_type=F32
    )


def right_inner(left_side, right_side):
    return lax.dot_general(
        left_side, right_side, (((left_side.ndim - 1,), (1,)), ((), ())), preferred_element_type=F32
    )


def left_inner(left_side, right_side):
    rows = tuple(range(left_side.ndim - 1))
    return lax.dot_general(
        left_side, right_side, ((rows, rows), ((), ())), preferred_element_type=F32
    )


def follow(value, *others):
    if not others:
        return value
    nothing = sum((o[(0,) * o.ndim].astype(F32) for o in others)) * 0.0
    return value + nothing.astype(value.dtype)


def whole(value):
    return lax.optimization_barrier(value)


def after(value, *others):
    return lax.optimization_barrier((value, *others))[0]


def spread(name, rows, gates={}):
    n = lax.axis_size("narrow")
    here = lax.axis_index("narrow")
    with jax.named_scope("spread_" + name):
        up, down = ([rows], [rows])
        for step in range(1, n):
            one, other = (
                follow(up[-1], *gates.get(step, ())),
                follow(down[-1], *gates.get(step, ())),
            )
            up.append(lax.ppermute(one, "narrow", [(k, k + 1) for k in range(step - 1, n - 1)]))
            down.append(lax.ppermute(other, "narrow", [(k, k - 1) for k in range(1, n - step + 1)]))
        parts = [rows] + [jnp.where(here >= s, up[s], down[n - s]) for s in range(1, n)]
        return (jnp.stack(parts), [(up[s], down[s]) for s in range(1, n)])


def sink(name, parts, gates={}, hops=(), until=None):
    n = lax.axis_size("narrow")
    hops = list(hops)
    with jax.named_scope("sink_" + name):
        for step in range(len(hops) + 1, until or n):
            one, other = (parts[step], parts[n - step])
            if hops:
                one = hops[-1][0].astype(F32) + one.astype(F32)
                other = hops[-1][1].astype(F32) + other.astype(F32)
            one, other = (follow(one, *gates.get(step, ())), follow(other, *gates.get(step, ())))
            up = lax.ppermute(one.astype(BF), "narrow", [(k, k + 1) for k in range(step)])
            down = lax.ppermute(
                other.astype(BF), "narrow", [(k, k - 1) for k in range(n - step, n)]
            )
            hops.append((up, down))
        if until:
            return (None, hops)
        return (up.astype(F32) + down.astype(F32) + parts[0].astype(F32), hops)


def norm_stats(features):
    center = features - jnp.mean(features, axis=-1, keepdims=True)
    rstd = lax.rsqrt(jnp.mean(center * center, axis=-1, keepdims=True) + EPSILON)
    return (center * rstd, rstd)


def norm_back(grad, xhat, rstd, gain):
    scaled = grad * gain
    return rstd * (
        scaled
        - jnp.mean(scaled, axis=-1, keepdims=True)
        - xhat * jnp.mean(scaled * xhat, axis=-1, keepdims=True)
    )


def norm_sums(grad, xhat):
    return jnp.stack([jnp.sum(grad * xhat, axis=0), jnp.sum(grad, axis=0)])


def score_block(queries, keys_in, allowed, score_scale):
    raw = jnp.einsum("iphe,iqhe->ihpq", queries, keys_in, preferred_element_type=F32)
    return jnp.where(allowed[:, None], raw * score_scale, MASKED)


def attend(queries, keys_in, values_in, allowed, score_scale):
    scores = score_block(queries, keys_in, allowed, score_scale)
    log_total = jax.nn.logsumexp(scores, axis=-1, keepdims=True)
    soft = jnp.exp(scores - log_total).astype(BF)
    mixture = jnp.einsum("ihpq,iqhe->iphe", soft, values_in, preferred_element_type=F32)
    return (mixture.astype(BF), log_total)


def attend_back(queries, keys_in, values_in, allowed, log_total, grad_mix, score_scale):
    soft = jnp.exp(score_block(queries, keys_in, allowed, score_scale) - log_total)
    grad_soft = jnp.einsum("iphe,iqhe->ihpq", grad_mix, values_in, preferred_element_type=F32)
    grad_values = jnp.einsum(
        "ihpq,iphe->iqhe", whole(soft.astype(BF)), grad_mix, preferred_element_type=F32
    )
    row_dot = jnp.sum(soft * grad_soft, axis=-1, keepdims=True)
    grad_scores = whole((soft * (grad_soft - row_dot) * score_scale).astype(BF))
    grad_queries = jnp.einsum("ihpq,iqhe->iphe", grad_scores, keys_in, preferred_element_type=F32)
    grad_keys = jnp.einsum("ihpq,iphe->iqhe", grad_scores, queries, preferred_element_type=F32)
    return (grad_queries.astype(BF), grad_keys, grad_values)


def body(
    tokens,
    out_grad,
    captions,
    image_blocks,
    caption_owner,
    norm_gains,
    norm_shifts,
    w_query,
    w_key,
    w_value,
    w_out,
    w_cross_query,
    w_cross_key,
    w_cross_value,
    w_cross_out,
    w_up,
    w_down,
):
    scale = HEAD_DIM ** (-0.5)
    n = lax.axis_size("narrow")
    here = lax.axis_index("narrow")
    width = w_query.shape[1]
    heads = width // HEAD_DIM
    part = PIX // CHUNKS
    chunks = [slice(c * part, (c + 1) * part) for c in range(CHUNKS)]
    image_of = (here - jnp.arange(n)) % n

    def rows_of(*pieces):
        return lax.all_gather(
            jnp.concatenate([p.astype(BF) for p in pieces], axis=1), "wide", axis=0, tiled=True
        )

    def columns_of(piece):
        return lax.all_gather(piece.astype(BF), "wide", axis=1, tiled=True)

    def to_rows(g):
        return lax.psum_scatter(g.astype(BF), "wide", scatter_dimension=0, tiled=True).astype(F32)

    def to_columns(g):
        return lax.psum_scatter(g.astype(BF), "wide", scatter_dimension=1, tiled=True).astype(F32)

    full_qkv = rows_of(w_query, w_key, w_value)
    residual0 = tokens.astype(F32)
    xhat1, rstd1 = norm_stats(residual0)
    own1 = (xhat1 * norm_gains[0] + norm_shifts[0]).astype(BF)
    full_out = columns_of(w_out)
    full_ckv = rows_of(w_cross_key, w_cross_value)
    full_cq = rows_of(w_cross_query)
    full_cout = columns_of(w_cross_out)
    full_up = rows_of(w_up)
    full_down = columns_of(w_down)
    normed1 = spread("n1", own1)[0]
    qkv = product(normed1, full_qkv).astype(BF)
    heads_of = lambda x: x.reshape(x.shape[:-1] + (x.shape[-1] // HEAD_DIM, HEAD_DIM))
    self_q, self_k, self_v = [heads_of(qkv[..., k * width : (k + 1) * width]) for k in range(3)]
    blocks = image_blocks[image_of]
    self_allowed = blocks[:, :, None] == blocks[:, None, :]
    self_mix, self_total = attend(self_q, self_k, self_v, self_allowed, scale)
    self_mix = self_mix.reshape(n, PIX, width)
    text = spread("text", follow(captions, normed1[1], normed1[n - 1]), {2: (self_mix,)})[0]
    text_count = text.shape[0] * text.shape[1]
    text_rows = text.reshape(text_count, text.shape[2])
    ckv = product(text_rows, full_ckv).astype(BF)
    cross_k = heads_of(ckv[None, :, :width])
    cross_v = heads_of(ckv[None, :, width:])
    owner = caption_owner[0].reshape(n, -1)[image_of].reshape(-1)
    part_image = jnp.repeat(image_of, part)
    cross_allowed = (part_image[:, None] == owner[None, :])[None]
    state = []
    for c, rows in enumerate(chunks):
        residual1 = (
            residual0[rows] + sink(f"r1_{c}", product(self_mix[:, rows], full_out).astype(BF))[0]
        )
        xhat2, rstd2 = norm_stats(residual1)
        state.append((residual1, xhat2, rstd2))
    normed2 = [
        spread(f"n2_{c}", (s[1] * norm_gains[1] + norm_shifts[1]).astype(BF))[0]
        for c, s in enumerate(state)
    ]
    grad_all, og_hops = spread("og", follow(out_grad, normed2[0][1], normed2[0][n - 1]))
    cross_q, cross_mix, cross_total, state3 = ([], [], [], [])
    for c in range(CHUNKS):
        if c > 0:
            normed2[c] = follow(normed2[c], sent, *og_hops[0])
        q = heads_of(product(normed2[c], full_cq).astype(BF).reshape(1, n * part, width))
        mix, total = attend(q, cross_k, cross_v, cross_allowed, scale)
        mix = mix.reshape(n, part, width)
        sent = whole(product(mix, full_cout).astype(BF))
        residual2 = state[c][0] + sink(f"r2_{c}", sent, {1: og_hops[1]} if c > 0 else {})[0]
        xhat3, rstd3 = norm_stats(residual2)
        cross_q.append(q)
        cross_mix.append(mix)
        cross_total.append(total)
        state3.append((residual2, xhat3, rstd3))
    normed3 = [
        spread(f"n3_{c}", (s[1] * norm_gains[2] + norm_shifts[2]).astype(BF))[0]
        for c, s in enumerate(state3)
    ]
    out_parts, acts, grad_hiddens, grad2, sums3 = ([], [], [], [], [])
    for c, rows in enumerate(chunks):
        hidden = product(normed3[c], full_up)
        grad_rows = grad_all[:, rows]
        acted, gelu_back = jax.vjp(jax.nn.gelu, hidden)
        acted = acted.astype(BF)
        grad_hidden = gelu_back(right_inner(grad_rows, full_down))[0].astype(BF)
        acts.append(acted)
        grad_hiddens.append(grad_hidden)
        grad_n3 = sink(f"d3_{c}", right_inner(grad_hidden, full_up).astype(BF))[0]
        residual2, xhat3, rstd3 = state3[c]
        sums3.append(norm_sums(grad_n3, xhat3))
        grad2.append(out_grad[rows].astype(F32) + norm_back(grad_n3, xhat3, rstd3, norm_gains[2]))
        out_parts.append(whole(product(acted, full_down).astype(BF)))
    cat = lambda xs: jnp.concatenate(xs, axis=1)
    acted, grad_hidden, n3 = (cat(acts), cat(grad_hiddens), cat(normed3))
    grad_down = left_inner(acted, cat([grad_all[:, rows] for rows in chunks]))
    grad_up = left_inner(n3, grad_hidden)
    e2, e2_hops = map(list, zip(*[spread(f"e2_{c}", g.astype(BF)) for c, g in enumerate(grad2)]))
    out_parts = [jnp.concatenate([p[k] for p in out_parts]) for k in range(n)]
    out_hops = sink("out", out_parts, {1: e2_hops[-1][1]}, until=n - 1)[1]
    own_down = to_columns(grad_down)
    own_up = to_rows(grad_up)
    e2[-1] = after(e2[-1], grad_down, grad_up)
    grad1, sums2, grad_cqs, grad_ck, grad_cv = ([], [], [], 0.0, 0.0)
    for c in range(CHUNKS):
        grad_mix = heads_of(right_inner(e2[c], full_cout).astype(BF).reshape(1, n * part, width))
        gq, gk, gv = attend_back(
            cross_q[c], cross_k, cross_v, cross_allowed, cross_total[c], grad_mix, scale
        )
        gq = gq.reshape(n, part, width)
        grad_cqs.append(gq)
        grad_ck = grad_ck + gk
        grad_cv = grad_cv + gv
        sent = whole(right_inner(gq if c == 0 else follow(gq, *out_hops[0]), full_cq).astype(BF))
        grad_n2 = sink(f"d2_{c}", sent, {1: out_hops[1]} if c > 0 else {})[0]
        _, xhat2, rstd2 = state[c]
        sums2.append(norm_sums(grad_n2, xhat2))
        grad1.append(grad2[c] + norm_back(grad_n2, xhat2, rstd2, norm_gains[1]))
    grad_cout = left_inner(cat(cross_mix), cat(e2))
    grad_cq = left_inner(cat(normed2), cat(grad_cqs))
    grad_ckv = jnp.concatenate(
        [grad_ck.reshape(text_count, width), grad_cv.reshape(text_count, width)], axis=1
    ).astype(BF)
    grad_text_part = whole(right_inner(grad_ckv, full_ckv).astype(BF).reshape(n, -1, text.shape[2]))
    grad_wckv = left_inner(text_rows, grad_ckv)
    e1, e1_hops = map(list, zip(*[spread(f"e1_{c}", g.astype(BF)) for c, g in enumerate(grad1)]))
    own_cout = to_columns(grad_cout)
    own_cq = to_rows(grad_cq)
    own_ckv = to_rows(grad_wckv)
    e1[-1] = after(e1[-1], grad_cout, grad_cq, grad_wckv)
    grad_mix = heads_of(cat([right_inner(e, full_out).astype(BF) for e in e1]))
    grad_mix = after(grad_mix, own_down, own_up)
    gq, gk, gv = attend_back(self_q, self_k, self_v, self_allowed, self_total, grad_mix, scale)
    out_sum, out_hops = sink("out", out_parts, {n - 1: e1_hops[-1][1]}, out_hops)
    block_out = (jnp.concatenate([s[0] for s in state3]) + out_sum).astype(BF)
    grad_text, text_hops = sink("text", grad_text_part, {1: e1_hops[-1][1], 2: (gq,)})
    grad_text = grad_text.astype(BF)
    grad_qkv = jnp.concatenate([g.astype(BF).reshape(n, PIX, width) for g in (gq, gk, gv)], axis=-1)
    grad_qkv = follow(grad_qkv, *text_hops[1])
    grad_out = left_inner(self_mix, cat(e1))
    grad_n1_part = whole(right_inner(grad_qkv, full_qkv).astype(BF))
    grad_n1 = sink("d1", grad_n1_part, {1: out_hops[-1]})[0]
    grad_wqkv = left_inner(normed1, after(grad_qkv, grad_n1_part))
    grad1 = jnp.concatenate(grad1)
    grad_n1 = after(grad_n1, own_cout, own_cq, own_ckv)
    grad_tokens = (grad1 + norm_back(grad_n1, xhat1, rstd1, norm_gains[0])).astype(BF)
    sums = lax.psum(
        jnp.stack([norm_sums(grad_n1, xhat1), sum(sums2), sum(sums3)]), ("wide", "narrow")
    )
    own_out = to_columns(grad_out)
    own_qkv = to_rows(grad_wqkv)
    return (
        block_out,
        grad_tokens,
        grad_text,
        sums[:, 0],
        sums[:, 1],
        own_qkv[:, :width],
        own_qkv[:, width : 2 * width],
        own_qkv[:, 2 * width :],
        own_out,
        own_cq,
        own_ckv[:, :width],
        own_ckv[:, width:],
        own_cout,
        own_up,
        own_down,
    )


def solution(mesh):
    in_specs = (
        P(("wide", "narrow"), None),
        P(("wide", "narrow"), None),
        P(("wide", "narrow"), None),
        P("wide", None),
        P("wide", None),
        P(),
        P(),
        P("wide", "narrow"),
        P("wide", "narrow"),
        P("wide", "narrow"),
        P("narrow", "wide"),
        P("wide", "narrow"),
        P("wide", "narrow"),
        P("wide", "narrow"),
        P("narrow", "wide"),
        P("wide", "narrow"),
        P("narrow", "wide"),
    )
    out_specs = (
        P(("wide", "narrow"), None),
        P(("wide", "narrow"), None),
        P(("wide", "narrow"), None),
        P(),
        P(),
        P("wide", "narrow"),
        P("wide", "narrow"),
        P("wide", "narrow"),
        P("narrow", "wide"),
        P("wide", "narrow"),
        P("wide", "narrow"),
        P("wide", "narrow"),
        P("narrow", "wide"),
        P("wide", "narrow"),
        P("narrow", "wide"),
    )
    return jax.shard_map(body, mesh=mesh, in_specs=in_specs, out_specs=out_specs, check_vma=False)
```

profile of v0, /device:TPU:0, one launch (start us, length us, event | category | flops | bytes accessed | tf_op | source)
XLA Modules:
  0.0 1216.4 jit_solution(7606526087314520934)
XLA Ops:
  27.7 21.0 %collective-permute-done = bf16[256,2048]{1,0:T(8,128)(2,1)S(1)} collective-permute-done((bf16[256,2048]{1,0:T(8,128)(2,1)S(1)}, bf16[256,2048]{1,0:T(8,128)(2,1)S(1)}, u32[]{:S(2)}, u32[]{:S(2)}) %collective-permute-start) | collective-permute-done | bytes 1048608 | tf_op jit(solution)/shard_map/spread_n1/ppermute | solution.py:59
  57.3 22.7 %collective-permute-done.2 = bf16[256,2048]{1,0:T(8,128)(2,1)} collective-permute-done((bf16[256,2048]{1,0:T(8,128)(2,1)}, bf16[256,2048]{1,0:T(8,128)(2,1)}, u32[]{:S(2)}, u32[]{:S(2)}) %collective-permute-start.2) | collective-permute-done | bytes 1048608 | tf_op jit(solution)/shard_map/spread_n1/ppermute | solution.py:60
  85.6 19.8 %collective-permute-done.3 = bf16[256,2048]{1,0:T(8,128)(2,1)S(1)} collective-permute-done((bf16[256,2048]{1,0:T(8,128)(2,1)}, bf16[256,2048]{1,0:T(8,128)(2,1)S(1)}, u32[]{:S(2)}, u32[]{:S(2)}) %collective-permute-start.3) | collective-permute-done | bytes 1048608 | tf_op jit(solution)/shard_map/spread_n1/ppermute | solution.py:60
  110.0 10.7 fusion.91
  199.6 11.8 collective-permute-start.12
  212.8 9.2 collective-permute-done.35
  247.2 8.5 collective-permute-done.19
  257.6 9.2 collective-permute-done.37
  280.1 9.3 collective-permute-done.38
  303.1 9.1 collective-permute-start.42
  328.0 9.1 convolution_convert_fusion.7
  352.4 14.3 %collective-permute-start.24 = (bf16[128,2048]{1,0:T(8,128)(2,1)}, bf16[128,2048]{1,0:T(8,128)(2,1)}, u32[]{:S(2)}, u32[]{:S(2)}) collective-permute-start(bf16[128,2048]{1,0:T(8,128)(2,1)} %get-tuple-element.112), channel_id=1, source_target_pairs={{0,1},{4,5},{8,9},{12,13},{16,17},{20,21},{24,25},{28,29}} | collective-permute-start | bytes 1572872 | tf_op jit(solution)/shard_map/sink_r2_0/ppermute | solution.py:75
  396.5 15.2 %collective-permute-start.25 = (bf16[128,2048]{1,0:T(8,128)(2,1)S(1)}, bf16[128,2048]{1,0:T(8,128)(2,1)S(1)}, u32[]{:S(2)}, u32[]{:S(2)}) collective-permute-start(bf16[128,2048]{1,0:T(8,128)(2,1)S(1)} %get-tuple-element.110), channel_id=1, source_target_pairs={{0,1},{1,2},{4,5},{5,6},{8,9},{9,10},{12,13},{13,14},{16,17},{17,1... | collective-permute-start | bytes 1572872 | tf_op jit(solution)/shard_map/sink_r2_0/ppermute | solution.py:75
  462.8 8.4 collective-permute-done.48
  497.8 9.2 collective-permute-done.59
  537.7 11.3 multiply_convert_fusion.3
  557.3 11.2 convolution_bitcast_fusion.1
  574.3 10.4 fusion.36
  584.7 9.3 fusion.114
  596.7 11.4 fusion.29
  608.2 8.6 fusion.117
  637.4 11.2 convolution_bitcast_fusion
  668.1 8.9 fusion.123
  704.6 9.3 collective-permute-done.74
  721.1 9.6 collective-permute-done.75
  794.8 8.2 fusion.227
  832.8 10.7 collective-permute-done.77
  971.4 9.7 convolution_convert_fusion
  1051.3 11.4 fusion.94
  1062.7 8.9 bitcast_convert_fusion
  1087.3 17.9 %collective-permute-done.124 = bf16[256,2048]{1,0:T(8,128)(2,1)S(1)} collective-permute-done((bf16[256,2048]{1,0:T(8,128)(2,1)S(1)}, bf16[256,2048]{1,0:T(8,128)(2,1)S(1)}, u32[]{:S(2)}, u32[]{:S(2)}) %collective-permute-start.124) | collective-permute-done | bytes 1048608 | tf_op jit(solution)/shard_map/sink_d1/ppermute | solution.py:75
  1163.2 40.0 %psum.7 = f32[3,2,2048]{2,0,1:T(4,128)S(1)} all-reduce(f32[3,2,2048]{2,0,1:T(4,128)S(1)} %pad_maximum_fusion.16), channel_id=1, replica_groups=mesh['wide'=8,'narrow'=4] {'wide','narrow'}, use_global_device_ids=true, to_apply=%region_44.45 | all-reduce | flops 12288 | bytes 98304 | tf_op jit(solution)/shard_map/psum | solution.py:296
  (943 shorter events, 787.3 us)
Async XLA Ops:
  7.2 102.8 %all-gather.8.cloned.1.call-start = ((), (), s32[]{:S(2)}) async-start(), calls=%async_computation.7 | async-start | bytes 7077888 | tf_op jit(solution)/shard_map/all_gather | solution.py:159
  11.6 119.0 %all-gather.10.cloned.1.call-start = ((), (), s32[]{:S(2)}) async-start(), calls=%async_computation.8 | async-start | bytes 2359296 | tf_op jit(solution)/shard_map/all_gather | solution.py:164
  12.4 299.8 %all-gather.14.cloned.1.call-start = ((), (), s32[]{:S(2)}) async-start(), calls=%async_computation.10 | async-start | bytes 2359296 | tf_op jit(solution)/shard_map/all_gather | solution.py:159
  14.4 313.6 %all-gather.12.cloned.1.call-start = ((), (), s32[]{:S(2)}) async-start(), calls=%async_computation.9 | async-start | bytes 9437184 | tf_op jit(solution)/shard_map/all_gather | solution.py:159
  17.0 330.0 %all-gather.16.cloned.1.call-start = ((), (), s32[]{:S(2)}) async-start(), calls=%async_computation.11 | async-start | bytes 2359296 | tf_op jit(solution)/shard_map/all_gather | solution.py:164
  18.8 518.8 %all-gather.18.cloned.1.call-start = ((), (), s32[]{:S(2)}) async-start(), calls=%async_computation.12 | async-start | bytes 9437184 | tf_op jit(solution)/shard_map/all_gather | solution.py:159
  20.0 554.2 %all-gather.20.cloned.1.call-start = ((), (), s32[]{:S(2)}) async-start(), calls=%async_computation.13 | async-start | bytes 9437184 | tf_op jit(solution)/shard_map/all_gather | solution.py:164
  108.5 61.7 %collective-permute-start.13 = (bf16[128,4096]{1,0:T(8,128)(2,1)}, bf16[128,4096]{1,0:T(8,128)(2,1)}, u32[]{:S(2)}, u32[]{:S(2)}) collective-permute-start(bf16[128,4096]{1,0:T(8,128)(2,1)} %broadcast_add_fusion.3), channel_id=1, source_target_pairs={{1,0},{2,1},{3,2},{5,4},{6,5},{7,6},{9,8},{10,9},{11,10},{13,12},{... | collective-permute-start | bytes 3145736 | tf_op jit(solution)/shard_map/spread_text/ppermute | solution.py:60
  150.2 853.7 %reduce-scatter.8.cloned.1.call-start = ((), (), s32[]{:S(2)}) async-start(), calls=%async_computation.14 | async-start | bytes 9437184 | tf_op jit(solution)/shard_map/reduce_scatter | solution.py:170
  174.8 36.7 %collective-permute-start.8 = (bf16[128,2048]{1,0:T(8,128)(2,1)S(1)}, bf16[128,2048]{1,0:T(8,128)(2,1)S(1)}, u32[]{:S(2)}, u32[]{:S(2)}) collective-permute-start(bf16[128,2048]{1,0:T(8,128)(2,1)S(1)} %get-tuple-element.122), channel_id=1, source_target_pairs={{0,1},{1,2},{2,3},{4,5},{5,6},{6,7},{8,9},{9,10},{10,11},{12,13},{... | collective-permute-start | bytes 1572872 | tf_op jit(solution)/shard_map/sink_r1_0/ppermute | solution.py:75
  179.2 33.6 %collective-permute-start.11 = (bf16[128,2048]{1,0:T(8,128)(2,1)S(1)}, bf16[128,2048]{1,0:T(8,128)(2,1)S(1)}, u32[]{:S(2)}, u32[]{:S(2)}) collective-permute-start(bf16[128,2048]{1,0:T(8,128)(2,1)S(1)} %get-tuple-element.123), channel_id=1, source_target_pairs={{1,0},{2,1},{3,2},{5,4},{6,5},{7,6},{9,8},{10,9},{11,10},{13,12},{... | collective-permute-start | bytes 1572872 | tf_op jit(solution)/shard_map/sink_r1_0/ppermute | solution.py:76
  199.6 34.5 %collective-permute-start.12 = (bf16[128,4096]{1,0:T(8,128)(2,1)}, bf16[128,4096]{1,0:T(8,128)(2,1)S(1)}, u32[]{:S(2)}, u32[]{:S(2)}) collective-permute-start(bf16[128,4096]{1,0:T(8,128)(2,1)} %broadcast_add_fusion.3), channel_id=1, source_target_pairs={{0,1},{1,2},{2,3},{4,5},{5,6},{6,7},{8,9},{9,10},{10,11},{12,13},{... | collective-permute-start | bytes 3145736 | tf_op jit(solution)/shard_map/spread_text/ppermute | solution.py:59
  232.8 34.1 %collective-permute-start.37 = (bf16[128,2048]{1,0:T(8,128)(2,1)S(1)}, bf16[128,2048]{1,0:T(8,128)(2,1)S(1)}, u32[]{:S(2)}, u32[]{:S(2)}) collective-permute-start(bf16[128,2048]{1,0:T(8,128)(2,1)S(1)} %get-tuple-element.160), channel_id=1, source_target_pairs={{1,0},{2,1},{3,2},{5,4},{6,5},{7,6},{9,8},{10,9},{11,10},{13,12},{... | collective-permute-start | bytes 1572872 | tf_op jit(solution)/shard_map/spread_n2_1/ppermute | solution.py:60
  234.1 34.0 %collective-permute-start.36 = (bf16[128,2048]{1,0:T(8,128)(2,1)S(1)}, bf16[128,2048]{1,0:T(8,128)(2,1)S(1)}, u32[]{:S(2)}, u32[]{:S(2)}) collective-permute-start(bf16[128,2048]{1,0:T(8,128)(2,1)S(1)} %get-tuple-element.160), channel_id=1, source_target_pairs={{0,1},{1,2},{2,3},{4,5},{5,6},{6,7},{8,9},{9,10},{10,11},{12,13},{... | collective-permute-start | bytes 1572872 | tf_op jit(solution)/shard_map/spread_n2_1/ppermute | solution.py:59
  245.5 48.9 %collective-permute-start.16 = (bf16[128,4096]{1,0:T(8,128)(2,1)S(1)}, bf16[128,4096]{1,0:T(8,128)(2,1)}, u32[]{:S(2)}, u32[]{:S(2)}) collective-permute-start(bf16[128,4096]{1,0:T(8,128)(2,1)S(1)} %get-tuple-element.143), channel_id=1, source_target_pairs={{1,2},{2,3},{5,6},{6,7},{9,10},{10,11},{13,14},{14,15},{17,18},{18... | collective-permute-start | bytes 3145736 | tf_op jit(solution)/shard_map/spread_text/ppermute | solution.py:59
  301.8 69.0 %collective-permute-start.43 = (bf16[256,2048]{1,0:T(8,128)(2,1)}, bf16[256,2048]{1,0:T(8,128)(2,1)}, u32[]{:S(2)}, u32[]{:S(2)}) collective-permute-start(bf16[256,2048]{1,0:T(8,128)(2,1)} %broadcast_add_fusion), channel_id=1, source_target_pairs={{1,0},{2,1},{3,2},{5,4},{6,5},{7,6},{9,8},{10,9},{11,10},{13,12},{... | collective-permute-start | bytes 3145736 | tf_op jit(solution)/shard_map/spread_og/ppermute | solution.py:60
  303.1 65.2 %collective-permute-start.42 = (bf16[256,2048]{1,0:T(8,128)(2,1)}, bf16[256,2048]{1,0:T(8,128)(2,1)}, u32[]{:S(2)}, u32[]{:S(2)}) collective-permute-start(bf16[256,2048]{1,0:T(8,128)(2,1)} %broadcast_add_fusion), channel_id=1, source_target_pairs={{0,1},{1,2},{2,3},{4,5},{5,6},{6,7},{8,9},{9,10},{10,11},{12,13},{... | collective-permute-start | bytes 3145736 | tf_op jit(solution)/shard_map/spread_og/ppermute | solution.py:59
  352.4 42.6 %collective-permute-start.24 = (bf16[128,2048]{1,0:T(8,128)(2,1)}, bf16[128,2048]{1,0:T(8,128)(2,1)}, u32[]{:S(2)}, u32[]{:S(2)}) collective-permute-start(bf16[128,2048]{1,0:T(8,128)(2,1)} %get-tuple-element.112), channel_id=1, source_target_pairs={{0,1},{4,5},{8,9},{12,13},{16,17},{20,21},{24,25},{28,29}} | collective-permute-start | bytes 1572872 | tf_op jit(solution)/shard_map/sink_r2_0/ppermute | solution.py:75
  432.6 54.0 %collective-permute-start.64 = (bf16[256,2048]{1,0:T(8,128)(2,1)}, bf16[256,2048]{1,0:T(8,128)(2,1)S(1)}, u32[]{:S(2)}, u32[]{:S(2)}) collective-permute-start(bf16[256,2048]{1,0:T(8,128)(2,1)} %collective-permute-done.45), channel_id=1, source_target_pairs={{1,0},{5,4},{9,8},{13,12},{17,16},{21,20},{25,24},{29,28}} | collective-permute-start | bytes 3145736 | tf_op jit(solution)/shard_map/spread_og/ppermute | solution.py:60
  444.0 65.0 %collective-permute-start.65 = (bf16[256,2048]{1,0:T(8,128)(2,1)}, bf16[256,2048]{1,0:T(8,128)(2,1)S(1)}, u32[]{:S(2)}, u32[]{:S(2)}) collective-permute-start(bf16[256,2048]{1,0:T(8,128)(2,1)} %collective-permute-done.44), channel_id=1, source_target_pairs={{2,3},{6,7},{10,11},{14,15},{18,19},{22,23},{26,27},{30,31}} | collective-permute-start | bytes 3145736 | tf_op jit(solution)/shard_map/spread_og/ppermute | solution.py:59
  568.5 438.2 %reduce-scatter.10.cloned.1.call-start = ((), (), s32[]{:S(2)}) async-start(), calls=%async_computation.15 | async-start | bytes 9437184 | tf_op jit(solution)/shard_map/reduce_scatter | solution.py:167
  648.7 434.8 %reduce-scatter.12.cloned.1.call-start = ((), (), s32[]{:S(2)}) async-start(), calls=%async_computation.16 | async-start | bytes 2359296 | tf_op jit(solution)/shard_map/reduce_scatter | solution.py:170
  735.7 78.8 %collective-permute-start.76 = (bf16[256,2048]{1,0:T(8,128)(2,1)}, bf16[256,2048]{1,0:T(8,128)(2,1)}, u32[]{:S(2)}, u32[]{:S(2)}) collective-permute-start(bf16[256,2048]{1,0:T(8,128)(2,1)} %fusion.318), channel_id=1, source_target_pairs={{0,1},{4,5},{8,9},{12,13},{16,17},{20,21},{24,25},{28,29}} | collective-permute-start | bytes 3145736 | tf_op jit(solution)/shard_map/sink_out/ppermute | solution.py:75
  740.5 74.0 %collective-permute-start.80 = (bf16[256,2048]{1,0:T(8,128)(2,1)}, bf16[256,2048]{1,0:T(8,128)(2,1)}, u32[]{:S(2)}, u32[]{:S(2)}) collective-permute-start(bf16[256,2048]{1,0:T(8,128)(2,1)} %fusion.317), channel_id=1, source_target_pairs={{3,2},{7,6},{11,10},{15,14},{19,18},{23,22},{27,26},{31,30}} | collective-permute-start | bytes 3145736 | tf_op jit(solution)/shard_map/sink_out/ppermute | solution.py:76
  788.2 64.2 %collective-permute-start.106 = (bf16[128,2048]{1,0:T(8,128)(2,1)}, bf16[128,2048]{1,0:T(8,128)(2,1)}, u32[]{:S(2)}, u32[]{:S(2)}) collective-permute-start(bf16[128,2048]{1,0:T(8,128)(2,1)} %get-tuple-element.80), channel_id=1, source_target_pairs={{0,1},{4,5},{8,9},{12,13},{16,17},{20,21},{24,25},{28,29}} | collective-permute-start | bytes 1572872 | tf_op jit(solution)/shard_map/sink_d2_0/ppermute | solution.py:75
  790.5 61.9 %collective-permute-start.109 = (bf16[128,2048]{1,0:T(8,128)(2,1)}, bf16[128,2048]{1,0:T(8,128)(2,1)}, u32[]{:S(2)}, u32[]{:S(2)}) collective-permute-start(bf16[128,2048]{1,0:T(8,128)(2,1)} %get-tuple-element.81), channel_id=1, source_target_pairs={{3,2},{7,6},{11,10},{15,14},{19,18},{23,22},{27,26},{31,30}} | collective-permute-start | bytes 1572872 | tf_op jit(solution)/shard_map/sink_d2_0/ppermute | solution.py:76
  814.4 270.9 %reduce-scatter.14.cloned.1.call-start = ((), (), s32[]{:S(2)}) async-start(), calls=%async_computation.17 | async-start | bytes 2359296 | tf_op jit(solution)/shard_map/reduce_scatter | solution.py:167
  880.4 245.2 %reduce-scatter.20.cloned.1.call-start = ((), (), s32[]{:S(2)}) async-start(), calls=%async_computation.20 | async-start | bytes 2359296 | tf_op jit(solution)/shard_map/reduce_scatter | solution.py:170
  970.2 178.2 %reduce-scatter.16.cloned.1.call-start = ((), (), s32[]{:S(2)}) async-start(), calls=%async_computation.18 | async-start | bytes 9437184 | tf_op jit(solution)/shard_map/reduce_scatter | solution.py:167
  970.9 236.3 %reduce-scatter.18.cloned.1.call-start = ((), (), s32[]{:S(2)}) async-start(), calls=%async_computation.19 | async-start | bytes 7077888 | tf_op jit(solution)/shard_map/reduce_scatter | solution.py:167
  987.6 84.0 %collective-permute-start.92 = (bf16[256,2048]{1,0:T(8,128)(2,1)}, bf16[256,2048]{1,0:T(8,128)(2,1)}, u32[]{:S(2)}, u32[]{:S(2)}) collective-permute-start(bf16[256,2048]{1,0:T(8,128)(2,1)} %add_convert_fusion.1), channel_id=1, source_target_pairs={{0,1},{1,2},{2,3},{4,5},{5,6},{6,7},{8,9},{9,10},{10,11},{12,13},{... | collective-permute-start | bytes 3145736 | tf_op jit(solution)/shard_map/sink_out/ppermute | solution.py:75
  1037.6 35.2 %collective-permute-start.93 = (bf16[256,2048]{1,0:T(8,128)(2,1)}, bf16[256,2048]{1,0:T(8,128)(2,1)}, u32[]{:S(2)}, u32[]{:S(2)}) collective-permute-start(bf16[256,2048]{1,0:T(8,128)(2,1)} %add_convert_fusion), channel_id=1, source_target_pairs={{1,0},{2,1},{3,2},{5,4},{6,5},{7,6},{9,8},{10,9},{11,10},{13,12},{... | collective-permute-start | bytes 3145736 | tf_op jit(solution)/shard_map/sink_out/ppermute | solution.py:76
  (311 other events, 6571.3 us)
Sparse Core Ops, SparseCore 0:
  11.7 48.1 all-gather.7
  62.3 28.0 all-gather.9
  92.9 27.7 all-gather.13
  122.4 54.2 all-gather.11
  178.4 28.0 all-gather.15
  208.3 54.2 all-gather.17
  264.5 55.8 all-gather.19
  568.6 74.8 reduce-scatter.7
  648.8 76.2 reduce-scatter.9
  814.5 40.9 reduce-scatter.11
  880.5 42.3 reduce-scatter.13
  970.3 40.5 reduce-scatter.19
  1014.3 71.4 reduce-scatter.15
  1089.0 61.7 reduce-scatter.17
where the time goes:
time: 1230 us; the launch traced here: 1220 us
  starting transfers between devices  335 us (27%)
  waiting for transfers between devices  309 us (25%)
  matrix products  250 us (20%)
  other arithmetic  162 us (13%)
  local copies, waits for them, and re-layouts  86.3 us (7%)
  blocking collectives  40 us (3%)
  between operations  33.3 us (3%)
    ppermute x33, waiting for transfers between devices, spread(): lax.ppermute(other, 'narrow', [(k, k - 1) for k in range(1, n - step + 1)])  169 us
    ppermute x33, starting transfers between devices, sink(): lax.ppermute(one.astype(BF), 'narrow', [(k, k + 1) for k in range(step)])  158 us
    ppermute x33, starting transfers between devices, spread(): lax.ppermute(one, 'narrow', [(k, k + 1) for k in range(step - 1, n - 1)])  89.9 us
    ppermute x33, waiting for transfers between devices, sink(): lax.ppermute(one.astype(BF), 'narrow', [(k, k + 1) for k in range(step)])  81.6 us
    dot_general x12, matrix products, right_inner(): lax.dot_general(left_side, right_side, (((left_side.ndim - 1,), (1,)), ((...  72.9 us
    dot_general x12, matrix products, product(): lax.dot_general(left_side, right_side, (((left_side.ndim - 1,), (0,)), ((...  68.6 us
    dot_general x7, matrix products, left_inner(): lax.dot_general(left_side, right_side, ((rows, rows), ((), ())), preferre...  52.4 us
    ppermute x33, starting transfers between devices, spread(): lax.ppermute(other, 'narrow', [(k, k - 1) for k in range(1, n - step + 1)])  43.1 us
  transfers between devices with their start and end apart: 146, of which 46 were waited for; matrix products, arithmetic and copies ran while one was open for 39% of the time, Pallas kernels for 0%

commit v1 on v0

--- a/solution.py
+++ b/solution.py
@@ -293,8 +293,11 @@
     grad1 = jnp.concatenate(grad1)
     grad_n1 = after(grad_n1, own_cout, own_cq, own_ckv)
     grad_tokens = (grad1 + norm_back(grad_n1, xhat1, rstd1, norm_gains[0])).astype(BF)
-    sums = lax.psum(
-        jnp.stack([norm_sums(grad_n1, xhat1), sum(sums2), sum(sums3)]), ("wide", "narrow")
+    sums = jnp.sum(
+        lax.all_gather(
+            jnp.stack([norm_sums(grad_n1, xhat1), sum(sums2), sum(sums3)]), ("wide", "narrow")
+        ),
+        axis=0,
     )
     own_out = to_columns(grad_out)
     own_qkv = to_rows(grad_wqkv)

time: 1230 us -> 1280 us (1.041)
  waiting for transfers between devices: 309 us -> 396 us
  blocking collectives: 40 us -> 0 us
    reduce_scatter x4, waiting for transfers between devices: 0.03 us -> 60.6 us  [to_rows(): lax.psum_scatter(g.astype(BF), 'wide', scatter_dimension=0, tiled=True)]
    psum x1 -> x0, blocking collectives: 40 us -> none  [body(): lax.psum(jnp.stack([norm_sums(grad_n1, xhat1), sum(sums2), sum(sums3)]),...]
    ppermute x33, waiting for transfers between devices: 81.6 us -> 95.2 us  [sink(): lax.ppermute(one.astype(BF), 'narrow', [(k, k + 1) for k in range(step)])]
  transfers between devices with their start and end apart: 146 -> 147, of which waited for: 46 -> 47; matrix products, arithmetic and copies ran while one was open for 39% -> 37% of each run, Pallas kernels for 0% -> 0%
where the time goes in v1:
time: 1280 us; the launch traced here: 1270 us
  waiting for transfers between devices  396 us (31%)
  starting transfers between devices  344 us (27%)
  matrix products  251 us (20%)
  other arithmetic  161 us (13%)
  local copies, waits for them, and re-layouts  86.9 us (7%)
  between operations  33.5 us (3%)
    ppermute x33, waiting for transfers between devices, spread(): lax.ppermute(other, 'narrow', [(k, k - 1) for k in range(1, n - step + 1)])  169 us
    ppermute x33, starting transfers between devices, sink(): lax.ppermute(one.astype(BF), 'narrow', [(k, k + 1) for k in range(step)])  166 us
    ppermute x33, waiting for transfers between devices, sink(): lax.ppermute(one.astype(BF), 'narrow', [(k, k + 1) for k in range(step)])  95.2 us
    ppermute x33, starting transfers between devices, spread(): lax.ppermute(one, 'narrow', [(k, k + 1) for k in range(step - 1, n - 1)])  91.7 us
    dot_general x12, matrix products, right_inner(): lax.dot_general(left_side, right_side, (((left_side.ndim - 1,), (1,)), ((...  69.6 us
    dot_general x12, matrix products, product(): lax.dot_general(left_side, right_side, (((left_side.ndim - 1,), (0,)), ((...  68.5 us
    reduce_scatter x4, waiting for transfers between devices, to_rows(): lax.psum_scatter(g.astype(BF), 'wide', scatter_dimension=0, tiled=True)  60.6 us
    dot_general x7, matrix products, left_inner(): lax.dot_general(left_side, right_side, ((rows, rows), ((), ())), preferre...  55.1 us
  transfers between devices with their start and end apart: 147, of which 47 were waited for; matrix products, arithmetic and copies ran while one was open for 37% of the time, Pallas kernels for 0%

profile of v1, /device:TPU:0, one launch (start us, length us, event | category | flops | bytes accessed | tf_op | source)
XLA Modules:
  0.0 1273.4 jit_solution(61746306979616526)
XLA Ops:
  27.7 21.0 %collective-permute-done = bf16[256,2048]{1,0:T(8,128)(2,1)S(1)} collective-permute-done((bf16[256,2048]{1,0:T(8,128)(2,1)S(1)}, bf16[256,2048]{1,0:T(8,128)(2,1)S(1)}, u32[]{:S(2)}, u32[]{:S(2)}) %collective-permute-start) | collective-permute-done | bytes 1048608 | tf_op jit(solution)/shard_map/spread_n1/ppermute | solution.py:59
  57.3 22.7 %collective-permute-done.2 = bf16[256,2048]{1,0:T(8,128)(2,1)} collective-permute-done((bf16[256,2048]{1,0:T(8,128)(2,1)}, bf16[256,2048]{1,0:T(8,128)(2,1)}, u32[]{:S(2)}, u32[]{:S(2)}) %collective-permute-start.2) | collective-permute-done | bytes 1048608 | tf_op jit(solution)/shard_map/spread_n1/ppermute | solution.py:60
  85.6 19.8 %collective-permute-done.3 = bf16[256,2048]{1,0:T(8,128)(2,1)S(1)} collective-permute-done((bf16[256,2048]{1,0:T(8,128)(2,1)}, bf16[256,2048]{1,0:T(8,128)(2,1)S(1)}, u32[]{:S(2)}, u32[]{:S(2)}) %collective-permute-start.3) | collective-permute-done | bytes 1048608 | tf_op jit(solution)/shard_map/spread_n1/ppermute | solution.py:60
  110.1 10.7 fusion.91
  199.7 11.8 collective-permute-start.12
  212.8 9.2 collective-permute-done.35
  257.6 9.2 collective-permute-done.37
  280.1 9.3 collective-permute-done.38
  303.1 9.1 collective-permute-start.42
  328.0 9.1 convolution_convert_fusion.7
  352.5 14.3 %collective-permute-start.24 = (bf16[128,2048]{1,0:T(8,128)(2,1)}, bf16[128,2048]{1,0:T(8,128)(2,1)}, u32[]{:S(2)}, u32[]{:S(2)}) collective-permute-start(bf16[128,2048]{1,0:T(8,128)(2,1)} %get-tuple-element.112), channel_id=1, source_target_pairs={{0,1},{4,5},{8,9},{12,13},{16,17},{20,21},{24,25},{28,29}} | collective-permute-start | bytes 1572872 | tf_op jit(solution)/shard_map/sink_r2_0/ppermute | solution.py:75
  396.6 15.2 %collective-permute-start.25 = (bf16[128,2048]{1,0:T(8,128)(2,1)S(1)}, bf16[128,2048]{1,0:T(8,128)(2,1)S(1)}, u32[]{:S(2)}, u32[]{:S(2)}) collective-permute-start(bf16[128,2048]{1,0:T(8,128)(2,1)S(1)} %get-tuple-element.110), channel_id=1, source_target_pairs={{0,1},{1,2},{4,5},{5,6},{8,9},{9,10},{12,13},{13,14},{16,17},{17,1... | collective-permute-start | bytes 1572872 | tf_op jit(solution)/shard_map/sink_r2_0/ppermute | solution.py:75
  497.8 9.2 collective-permute-done.59
  537.8 11.4 multiply_convert_fusion.3
  557.3 11.2 convolution_bitcast_fusion.1
  574.3 10.4 fusion.36
  584.8 9.3 fusion.114
  596.8 11.4 fusion.29
  608.2 8.6 fusion.117
  637.4 11.2 convolution_bitcast_fusion
  668.2 8.8 fusion.123
  704.2 9.5 collective-permute-done.74
  720.9 9.6 collective-permute-done.75
  934.1 9.6 convolution_convert_fusion
  953.5 12.0 collective-permute-start.92
  977.0 15.1 %collective-permute-done.118 = bf16[128,2048]{1,0:T(8,128)(2,1)S(1)} collective-permute-done((bf16[128,2048]{1,0:T(8,128)(2,1)}, bf16[128,2048]{1,0:T(8,128)(2,1)S(1)}, u32[]{:S(2)}, u32[]{:S(2)}) %collective-permute-start.118) | collective-permute-done | bytes 524320 | tf_op jit(solution)/shard_map/spread_e1_1/ppermute | solution.py:60
  1060.8 10.0 fusion.94
  1076.7 14.1 %collective-permute-done.124 = bf16[256,2048]{1,0:T(8,128)(2,1)S(1)} collective-permute-done((bf16[256,2048]{1,0:T(8,128)(2,1)S(1)}, bf16[256,2048]{1,0:T(8,128)(2,1)S(1)}, u32[]{:S(2)}, u32[]{:S(2)}) %collective-permute-start.124) | collective-permute-done | bytes 1048608 | tf_op jit(solution)/shard_map/sink_d1/ppermute | solution.py:75
  1101.2 13.5 %collective-permute-done.125 = bf16[256,2048]{1,0:T(8,128)(2,1)S(1)} collective-permute-done((bf16[256,2048]{1,0:T(8,128)(2,1)S(1)}, bf16[256,2048]{1,0:T(8,128)(2,1)S(1)}, u32[]{:S(2)}, u32[]{:S(2)}) %collective-permute-start.125) | collective-permute-done | bytes 1048608 | tf_op jit(solution)/shard_map/sink_d1/ppermute | solution.py:75
  1146.2 11.5 bitcast_convert_fusion
  1191.6 8.5 all-gather.24.cloned.1.call-done
  1203.5 60.5 %reduce-scatter.18.cloned.1.call-done = bf16[256,1536]{1,0:T(8,128)(2,1)} async-done(((bf16[2048,1536]{1,0:T(8,128)(2,1)}), bf16[256,1536]{1,0:T(8,128)(2,1)}) %reduce-scatter.18.cloned.1.call-update) | async-done | bytes 786448 | tf_op jit(solution)/shard_map/reduce_scatter | solution.py:167
  (929 shorter events, 813.0 us)
Async XLA Ops:
  7.2 102.8 %all-gather.10.cloned.1.call-start = ((), (), s32[]{:S(2)}) async-start(), calls=%async_computation.7 | async-start | bytes 7077888 | tf_op jit(solution)/shard_map/all_gather | solution.py:159
  11.6 119.0 %all-gather.12.cloned.1.call-start = ((), (), s32[]{:S(2)}) async-start(), calls=%async_computation.8 | async-start | bytes 2359296 | tf_op jit(solution)/shard_map/all_gather | solution.py:164
  12.4 299.8 %all-gather.16.cloned.1.call-start = ((), (), s32[]{:S(2)}) async-start(), calls=%async_computation.10 | async-start | bytes 2359296 | tf_op jit(solution)/shard_map/all_gather | solution.py:159
  14.4 313.7 %all-gather.14.cloned.1.call-start = ((), (), s32[]{:S(2)}) async-start(), calls=%async_computation.9 | async-start | bytes 9437184 | tf_op jit(solution)/shard_map/all_gather | solution.py:159
  17.0 330.0 %all-gather.18.cloned.1.call-start = ((), (), s32[]{:S(2)}) async-start(), calls=%async_computation.11 | async-start | bytes 2359296 | tf_op jit(solution)/shard_map/all_gather | solution.py:164
  18.8 518.9 %all-gather.20.cloned.1.call-start = ((), (), s32[]{:S(2)}) async-start(), calls=%async_computation.12 | async-start | bytes 9437184 | tf_op jit(solution)/shard_map/all_gather | solution.py:159
  20.0 554.3 %all-gather.22.cloned.1.call-start = ((), (), s32[]{:S(2)}) async-start(), calls=%async_computation.13 | async-start | bytes 9437184 | tf_op jit(solution)/shard_map/all_gather | solution.py:164
  108.5 61.8 %collective-permute-start.13 = (bf16[128,4096]{1,0:T(8,128)(2,1)}, bf16[128,4096]{1,0:T(8,128)(2,1)}, u32[]{:S(2)}, u32[]{:S(2)}) collective-permute-start(bf16[128,4096]{1,0:T(8,128)(2,1)} %broadcast_add_fusion.3), channel_id=1, source_target_pairs={{1,0},{2,1},{3,2},{5,4},{6,5},{7,6},{9,8},{10,9},{11,10},{13,12},{... | collective-permute-start | bytes 3145736 | tf_op jit(solution)/shard_map/spread_text/ppermute | solution.py:60
  150.2 859.6 %reduce-scatter.8.cloned.1.call-start = ((), (), s32[]{:S(2)}) async-start(), calls=%async_computation.14 | async-start | bytes 9437184 | tf_op jit(solution)/shard_map/reduce_scatter | solution.py:170
  174.8 36.6 %collective-permute-start.8 = (bf16[128,2048]{1,0:T(8,128)(2,1)S(1)}, bf16[128,2048]{1,0:T(8,128)(2,1)S(1)}, u32[]{:S(2)}, u32[]{:S(2)}) collective-permute-start(bf16[128,2048]{1,0:T(8,128)(2,1)S(1)} %get-tuple-element.122), channel_id=1, source_target_pairs={{0,1},{1,2},{2,3},{4,5},{5,6},{6,7},{8,9},{9,10},{10,11},{12,13},{... | collective-permute-start | bytes 1572872 | tf_op jit(solution)/shard_map/sink_r1_0/ppermute | solution.py:75
  199.7 34.5 %collective-permute-start.12 = (bf16[128,4096]{1,0:T(8,128)(2,1)}, bf16[128,4096]{1,0:T(8,128)(2,1)S(1)}, u32[]{:S(2)}, u32[]{:S(2)}) collective-permute-start(bf16[128,4096]{1,0:T(8,128)(2,1)} %broadcast_add_fusion.3), channel_id=1, source_target_pairs={{0,1},{1,2},{2,3},{4,5},{5,6},{6,7},{8,9},{9,10},{10,11},{12,13},{... | collective-permute-start | bytes 3145736 | tf_op jit(solution)/shard_map/spread_text/ppermute | solution.py:59
  232.8 34.1 %collective-permute-start.37 = (bf16[128,2048]{1,0:T(8,128)(2,1)S(1)}, bf16[128,2048]{1,0:T(8,128)(2,1)S(1)}, u32[]{:S(2)}, u32[]{:S(2)}) collective-permute-start(bf16[128,2048]{1,0:T(8,128)(2,1)S(1)} %get-tuple-element.160), channel_id=1, source_target_pairs={{1,0},{2,1},{3,2},{5,4},{6,5},{7,6},{9,8},{10,9},{11,10},{13,12},{... | collective-permute-start | bytes 1572872 | tf_op jit(solution)/shard_map/spread_n2_1/ppermute | solution.py:60
  245.5 48.9 %collective-permute-start.16 = (bf16[128,4096]{1,0:T(8,128)(2,1)S(1)}, bf16[128,4096]{1,0:T(8,128)(2,1)}, u32[]{:S(2)}, u32[]{:S(2)}) collective-permute-start(bf16[128,4096]{1,0:T(8,128)(2,1)S(1)} %get-tuple-element.143), channel_id=1, source_target_pairs={{1,2},{2,3},{5,6},{6,7},{9,10},{10,11},{13,14},{14,15},{17,18},{18... | collective-permute-start | bytes 3145736 | tf_op jit(solution)/shard_map/spread_text/ppermute | solution.py:59
  301.8 69.1 %collective-permute-start.43 = (bf16[256,2048]{1,0:T(8,128)(2,1)}, bf16[256,2048]{1,0:T(8,128)(2,1)}, u32[]{:S(2)}, u32[]{:S(2)}) collective-permute-start(bf16[256,2048]{1,0:T(8,128)(2,1)} %broadcast_add_fusion), channel_id=1, source_target_pairs={{1,0},{2,1},{3,2},{5,4},{6,5},{7,6},{9,8},{10,9},{11,10},{13,12},{... | collective-permute-start | bytes 3145736 | tf_op jit(solution)/shard_map/spread_og/ppermute | solution.py:60
  303.1 65.3 %collective-permute-start.42 = (bf16[256,2048]{1,0:T(8,128)(2,1)}, bf16[256,2048]{1,0:T(8,128)(2,1)}, u32[]{:S(2)}, u32[]{:S(2)}) collective-permute-start(bf16[256,2048]{1,0:T(8,128)(2,1)} %broadcast_add_fusion), channel_id=1, source_target_pairs={{0,1},{1,2},{2,3},{4,5},{5,6},{6,7},{8,9},{9,10},{10,11},{12,13},{... | collective-permute-start | bytes 3145736 | tf_op jit(solution)/shard_map/spread_og/ppermute | solution.py:59
  352.5 42.6 %collective-permute-start.24 = (bf16[128,2048]{1,0:T(8,128)(2,1)}, bf16[128,2048]{1,0:T(8,128)(2,1)}, u32[]{:S(2)}, u32[]{:S(2)}) collective-permute-start(bf16[128,2048]{1,0:T(8,128)(2,1)} %get-tuple-element.112), channel_id=1, source_target_pairs={{0,1},{4,5},{8,9},{12,13},{16,17},{20,21},{24,25},{28,29}} | collective-permute-start | bytes 1572872 | tf_op jit(solution)/shard_map/sink_r2_0/ppermute | solution.py:75
  432.6 54.1 %collective-permute-start.64 = (bf16[256,2048]{1,0:T(8,128)(2,1)}, bf16[256,2048]{1,0:T(8,128)(2,1)S(1)}, u32[]{:S(2)}, u32[]{:S(2)}) collective-permute-start(bf16[256,2048]{1,0:T(8,128)(2,1)} %collective-permute-done.45), channel_id=1, source_target_pairs={{1,0},{5,4},{9,8},{13,12},{17,16},{21,20},{25,24},{29,28}} | collective-permute-start | bytes 3145736 | tf_op jit(solution)/shard_map/spread_og/ppermute | solution.py:60
  444.1 65.0 %collective-permute-start.65 = (bf16[256,2048]{1,0:T(8,128)(2,1)}, bf16[256,2048]{1,0:T(8,128)(2,1)S(1)}, u32[]{:S(2)}, u32[]{:S(2)}) collective-permute-start(bf16[256,2048]{1,0:T(8,128)(2,1)} %collective-permute-done.44), channel_id=1, source_target_pairs={{2,3},{6,7},{10,11},{14,15},{18,19},{22,23},{26,27},{30,31}} | collective-permute-start | bytes 3145736 | tf_op jit(solution)/shard_map/spread_og/ppermute | solution.py:59
  568.6 443.9 %reduce-scatter.10.cloned.1.call-start = ((), (), s32[]{:S(2)}) async-start(), calls=%async_computation.15 | async-start | bytes 9437184 | tf_op jit(solution)/shard_map/reduce_scatter | solution.py:167
  648.6 477.9 %reduce-scatter.12.cloned.1.call-start = ((), (), s32[]{:S(2)}) async-start(), calls=%async_computation.16 | async-start | bytes 2359296 | tf_op jit(solution)/shard_map/reduce_scatter | solution.py:170
  735.5 79.1 %collective-permute-start.76 = (bf16[256,2048]{1,0:T(8,128)(2,1)}, bf16[256,2048]{1,0:T(8,128)(2,1)}, u32[]{:S(2)}, u32[]{:S(2)}) collective-permute-start(bf16[256,2048]{1,0:T(8,128)(2,1)} %fusion.318), channel_id=1, source_target_pairs={{0,1},{4,5},{8,9},{12,13},{16,17},{20,21},{24,25},{28,29}} | collective-permute-start | bytes 3145736 | tf_op jit(solution)/shard_map/sink_out/ppermute | solution.py:75
  740.4 74.2 %collective-permute-start.80 = (bf16[256,2048]{1,0:T(8,128)(2,1)}, bf16[256,2048]{1,0:T(8,128)(2,1)}, u32[]{:S(2)}, u32[]{:S(2)}) collective-permute-start(bf16[256,2048]{1,0:T(8,128)(2,1)} %fusion.317), channel_id=1, source_target_pairs={{3,2},{7,6},{11,10},{15,14},{19,18},{23,22},{27,26},{31,30}} | collective-permute-start | bytes 3145736 | tf_op jit(solution)/shard_map/sink_out/ppermute | solution.py:76
  788.2 64.3 %collective-permute-start.106 = (bf16[128,2048]{1,0:T(8,128)(2,1)}, bf16[128,2048]{1,0:T(8,128)(2,1)}, u32[]{:S(2)}, u32[]{:S(2)}) collective-permute-start(bf16[128,2048]{1,0:T(8,128)(2,1)} %get-tuple-element.80), channel_id=1, source_target_pairs={{0,1},{4,5},{8,9},{12,13},{16,17},{20,21},{24,25},{28,29}} | collective-permute-start | bytes 1572872 | tf_op jit(solution)/shard_map/sink_d2_0/ppermute | solution.py:75
  790.4 62.0 %collective-permute-start.109 = (bf16[128,2048]{1,0:T(8,128)(2,1)}, bf16[128,2048]{1,0:T(8,128)(2,1)}, u32[]{:S(2)}, u32[]{:S(2)}) collective-permute-start(bf16[128,2048]{1,0:T(8,128)(2,1)} %get-tuple-element.81), channel_id=1, source_target_pairs={{3,2},{7,6},{11,10},{15,14},{19,18},{23,22},{27,26},{31,30}} | collective-permute-start | bytes 1572872 | tf_op jit(solution)/shard_map/sink_d2_0/ppermute | solution.py:76
  826.2 302.1 %reduce-scatter.14.cloned.1.call-start = ((), (), s32[]{:S(2)}) async-start(), calls=%async_computation.17 | async-start | bytes 2359296 | tf_op jit(solution)/shard_map/reduce_scatter | solution.py:167
  881.6 262.7 %reduce-scatter.16.cloned.1.call-start = ((), (), s32[]{:S(2)}) async-start(), calls=%async_computation.18 | async-start | bytes 9437184 | tf_op jit(solution)/shard_map/reduce_scatter | solution.py:167
  943.8 226.6 %reduce-scatter.20.cloned.1.call-start = ((), (), s32[]{:S(2)}) async-start(), calls=%async_computation.20 | async-start | bytes 2359296 | tf_op jit(solution)/shard_map/reduce_scatter | solution.py:170
  953.5 87.1 %collective-permute-start.92 = (bf16[256,2048]{1,0:T(8,128)(2,1)}, bf16[256,2048]{1,0:T(8,128)(2,1)}, u32[]{:S(2)}, u32[]{:S(2)}) collective-permute-start(bf16[256,2048]{1,0:T(8,128)(2,1)} %add_convert_fusion.1), channel_id=1, source_target_pairs={{0,1},{1,2},{2,3},{4,5},{5,6},{6,7},{8,9},{9,10},{10,11},{12,13},{... | collective-permute-start | bytes 3145736 | tf_op jit(solution)/shard_map/sink_out/ppermute | solution.py:75
  968.2 73.6 %collective-permute-start.93 = (bf16[256,2048]{1,0:T(8,128)(2,1)}, bf16[256,2048]{1,0:T(8,128)(2,1)}, u32[]{:S(2)}, u32[]{:S(2)}) collective-permute-start(bf16[256,2048]{1,0:T(8,128)(2,1)} %add_convert_fusion), channel_id=1, source_target_pairs={{1,0},{2,1},{3,2},{5,4},{6,5},{7,6},{9,8},{10,9},{11,10},{13,12},{... | collective-permute-start | bytes 3145736 | tf_op jit(solution)/shard_map/sink_out/ppermute | solution.py:76
  973.3 59.4 %collective-permute-start.122 = (bf16[128,4096]{1,0:T(8,128)(2,1)}, bf16[128,4096]{1,0:T(8,128)(2,1)}, u32[]{:S(2)}, u32[]{:S(2)}) collective-permute-start(bf16[128,4096]{1,0:T(8,128)(2,1)} %get-tuple-element.71), channel_id=1, source_target_pairs={{3,2},{7,6},{11,10},{15,14},{19,18},{23,22},{27,26},{31,30}} | collective-permute-start | bytes 3145736 | tf_op jit(solution)/shard_map/sink_text/ppermute | solution.py:76
  1101.2 99.0 %all-gather.24.cloned.1.call-start = ((), (), s32[]{:S(2)}) async-start(), calls=%async_computation.21 | async-start | bytes 1622016 | tf_op jit(solution)/shard_map/all_gather | solution.py:297
  1146.2 117.9 %reduce-scatter.18.cloned.1.call-start = ((), (), s32[]{:S(2)}) async-start(), calls=%async_computation.19 | async-start | bytes 7077888 | tf_op jit(solution)/shard_map/reduce_scatter | solution.py:167
  (303 other events, 6655.8 us)
Sparse Core Ops, SparseCore 0:
  11.7 48.1 all-gather.9
  62.3 28.0 all-gather.11
  92.9 27.7 all-gather.15
  122.4 54.2 all-gather.13
  178.4 28.0 all-gather.17
  208.3 54.2 all-gather.19
  264.5 55.8 all-gather.21
  568.7 74.8 reduce-scatter.7
  648.7 76.2 reduce-scatter.9
  826.3 40.8 reduce-scatter.11
  881.8 44.3 reduce-scatter.13
  943.9 73.6 reduce-scatter.15
  1101.3 40.2 reduce-scatter.19
  1146.3 53.8 all-gather.23
  1203.4 60.6 reduce-scatter.17
